TPU v7x, 32 devices: a whole 2x2x4 slice. The times are simulated.
32 devices in a mesh: seg: 4 (over y, core), vid: 4 (over z), tp: 2 (over x).
Axes of the slice: x: 2, y: 2, z: 4, core: 2. Of those that a mesh axis runs over, the one named last changes fastest.
Arguments:
- tokens: bfloat16 [4, 2048, 2048], P('vid', 'seg', 'tp'), may hold values from -400 to 400
- key_weight: bfloat16 [2048, 2048], P('vid', 'tp'), may hold values from -0.125 to 0.125
- query_weight: bfloat16 [2048, 2048], P('vid', 'tp'), may hold values from -0.125 to 0.125
- latent_queries: bfloat16 [128, 2048], P(None, 'tp'), may hold values from -400 to 400
- init_memory: float32 [4, 128, 2048], P('vid', None, 'tp'), may hold values from -6 to 6
- forget: float32 [4, 4, 2048], P('vid', 'seg', 'tp'), may hold values from 0 to 1
Outputs:
- mixed: bfloat16 [4, 2048, 2048], P('vid', 'seg', 'tp')
- memory: float32 [4, 512, 2048], P('vid', 'seg', 'tp')
All inputs are finite; a program needn't handle non-finite values.
Results may differ from a plain program's by a relative error of at most 0.015.
The roundings to bfloat16 on the way count: a program that leaves them out, or rounds other values in their place, can miss the bound.
Values may be sent and summed in bfloat16 or wider, within the bound.
A program may use at most 64 MiB of HBM per device.

v0:
```python
import functools

import jax
import jax.numpy as jnp
from jax import lax
from jax.experimental import pallas as pl
from jax.experimental.pallas import tpu as pltpu
from jax.sharding import PartitionSpec as P

HEAD = 128


def from_behind(block, axis, distance):
    devices = range(lax.axis_size(axis))
    route = [(i - distance, i) for i in devices if i - distance in devices]
    return lax.ppermute(block, axis, route)


def trailing_softmax(scores):
    top = jnp.max(scores, axis=-1, keepdims=True)
    expo = jnp.exp(scores - top)
    return expo / jnp.sum(expo, axis=-1, keepdims=True)


def add_rows(left, piece):
    return jnp.dot(left, piece, preferred_element_type=jnp.float32)


def shards(tokens, key_weight, query_weight, latent_queries, init_memory, forget):
    local = tokens[0]
    width = local.shape[1]
    heads = width // HEAD
    latents = latent_queries.shape[0]
    whole = lax.all_gather(local, "tp", axis=1, tiled=True)

    def add_one(piece):
        return add_rows(whole, piece)

    keys_full = add_one(lax.all_gather(key_weight, "vid", axis=0, tiled=True))
    queries_full = add_one(lax.all_gather(query_weight, "vid", axis=0, tiled=True))
    scale = 1.0 / jnp.sqrt(jnp.float32(HEAD))
    keys = keys_full.astype(jnp.bfloat16).reshape(-1, heads, HEAD)
    queries = queries_full.astype(jnp.bfloat16).reshape(-1, heads, HEAD)
    values = local.reshape(-1, heads, HEAD)
    latent = latent_queries.reshape(latents, heads, HEAD)
    scores = jnp.einsum("mhe,the->hmt", latent, keys, preferred_element_type=jnp.float32) * scale
    weight_params = trailing_softmax(scores).astype(jnp.bfloat16)
    update = jnp.einsum(
        "hmt,the->mhe", weight_params, values, preferred_element_type=jnp.float32
    ).reshape(latents, width)
    retain = forget[0]
    initial_memory = init_memory[0]
    first = lax.axis_index("seg") == 0

    def turn(step, memory_now):
        received = from_behind(retain * memory_now + update, "seg", 1)
        return jnp.where(first, initial_memory, received)

    memory_in = lax.fori_loop(0, lax.axis_size("seg") - 1, turn, initial_memory)
    memory_out = retain * memory_in + update
    grouped = memory_in.reshape(latents, heads, HEAD)
    normed = grouped * lax.rsqrt(jnp.mean(grouped * grouped, axis=-1, keepdims=True) + 1e-06)
    read_scores = (
        jnp.einsum(
            "the,mhe->htm", queries, normed.astype(jnp.bfloat16), preferred_element_type=jnp.float32
        )
        * scale
    )
    read_weights = trailing_softmax(read_scores).astype(jnp.bfloat16)
    read = jnp.einsum(
        "htm,mhe->the",
        read_weights,
        grouped.astype(jnp.bfloat16),
        preferred_element_type=jnp.float32,
    )
    mixed = (local.astype(jnp.float32) + read.reshape(-1, width)).astype(jnp.bfloat16)
    return (mixed[None], memory_out[None])


SPLITS = 2
CORES = 2


def softmax_rows(scores):
    top = jnp.max(scores, axis=-1, keepdims=True)
    expo = jnp.exp(scores - top)
    return (expo * (1.0 / jnp.sum(expo, axis=-1, keepdims=True))).astype(jnp.bfloat16)


def fused_kernel(
    segs, vids, tps,
    tokens, key_w, query_w, latent, init_memory, forget,
    mixed, memory_out,
    weights, tok, keys, queries, memory_in, update, partial,
    load_sem, tok_send, tok_recv, z_send, z_recv, y_send, y_recv, d_send, d_recv, m_send, m_recv,
):
    chips = segs // CORES
    s, z, t = lax.axis_index("seg"), lax.axis_index("vid"), lax.axis_index("tp")
    y, core = s // CORES, s % CORES
    partner = y * CORES + (1 - core)
    width = tokens.shape[1]
    heads = width // HEAD
    rows = weights.shape[2] * weights.shape[3]
    streams = range(2 * SPLITS)
    sides = (1, -1)

    def remote(src, dst, send, recv, device):
        return pltpu.make_async_remote_copy(
            src_ref=src, dst_ref=dst, send_sem=send, recv_sem=recv,
            device_id=device, device_id_type=pl.DeviceIdType.MESH,
        )

    def z_copy(k, source, side):
        block = weights.at[k, source, s]
        return remote(block, block, z_send.at[k, source, (1 - side) // 2], z_recv.at[k, source], {"vid": z + side})

    def y_copy(k, source, chip, side):
        block = weights.at[k, source, chip * CORES + core]
        return remote(
            block, block, y_send.at[k, source, chip, (1 - side) // 2], y_recv.at[k, source, chip], {"seg": s + side * CORES}
        )

    def d_copy(k, source, chip, owner):
        block = weights.at[k, source, chip * CORES + owner]
        return remote(block, block, d_send.at[k, source, chip], d_recv.at[k, source, chip], {"seg": partner})

    def m_copy(h):
        cols = pl.ds(h * HEAD, HEAD)
        return remote(memory_out.at[:, cols], memory_in.at[:, cols], m_send.at[h], m_recv.at[h], {"seg": s + 1})

    def inside(index, size):
        return (index >= 0) & (index < size)

    def flag(condition):
        return jnp.where(condition, 1, 0).astype(jnp.int32)

    tok_load = pltpu.make_async_copy(tokens, tok.at[t], load_sem.at[0])
    first_memory = pltpu.make_async_copy(init_memory, memory_in, load_sem.at[1])
    loads = [
        pltpu.make_async_copy((key_w, query_w)[k // SPLITS].at[k % SPLITS], weights.at[k, z], load_sem.at[2 + k])
        for k in streams
    ]
    key_streams, query_streams = streams[:SPLITS], streams[SPLITS:]
    for load in loads[:SPLITS] + [tok_load] + loads[SPLITS:]:
        load.start()

    @pl.when(s == 0)
    def _():
        first_memory.start()

    barrier = pltpu.get_barrier_semaphore()
    greeted = [
        (z + 1 < vids, {"vid": z + 1}),
        (z > 0, {"vid": z - 1}),
        (y + 1 < chips, {"seg": s + CORES}),
        (y > 0, {"seg": s - CORES}),
        ((core == 1) & (y + 1 < chips), {"seg": s + 1}),
        ((core == 0) & (y > 0), {"seg": s - 1}),
        (s >= 0, {"seg": partner}),
        (s >= 0, {"tp": 1 - t}),
    ]
    count = 0
    for condition, device in greeted:
        count = count + flag(condition)

        @pl.when(condition)
        def _(device=device):
            pl.semaphore_signal(barrier, inc=1, device_id=device, device_id_type=pl.DeviceIdType.MESH)

    pl.semaphore_wait(barrier, count)

    def own_sends(k):
        for side in sides:
            @pl.when(inside(z + side, vids))
            def _(side=side):
                z_copy(k, z, side).start()

    tok_copy = remote(tok.at[t], tok.at[t], tok_send, tok_recv, {"tp": 1 - t})
    for k in key_streams:
        loads[k].wait()
        own_sends(k)
    tok_load.wait()
    tok_copy.start()
    for k in query_streams:
        loads[k].wait()

    def each_source(distance, action):
        for side in sides:
            source = z - side * distance

            @pl.when(inside(source, vids))
            def _(source=source, side=side):
                action(source, side)

    def arrive_z(k, distance):
        def action(source, side):
            z_copy(k, source, side).wait_recv()

            @pl.when(inside(z + side, vids))
            def _():
                z_copy(k, source, side).start()

            for step in sides:
                @pl.when(inside(y + step, chips))
                def _(step=step):
                    y_copy(k, source, y, step).start()

            d_copy(k, source, y, core).start()

        each_source(distance, action)

    def each_chip(action):
        for gap in range(1, chips):
            for step in sides:
                chip = y - step * gap

                @pl.when(inside(chip, chips))
                def _(chip=chip, step=step):
                    action(chip, step)

    def arrive_y(k, distance):
        def action(source, side):
            def one(chip, step):
                y_copy(k, source, chip, step).wait_recv()

                @pl.when(inside(y + step, chips))
                def _():
                    y_copy(k, source, chip, step).start()

                d_copy(k, source, chip, core).start()

            each_chip(one)

        each_source(distance, action)

    last = jnp.where(2 * z < vids, vids - 1, 0)

    def arrive_d(k, distance, final=None):
        def action(source, side):
            def take():
                for chip in range(chips):
                    d_copy(k, source, chip, 1 - core).wait_recv()

            if final is None:
                take()
            else:
                pl.when((source == last) == final)(take)

        each_source(distance, action)

    tile = 2 * HEAD

    def product(first, sources, at):
        total = None
        for source in sources:
            begin = source * rows * SPLITS
            for part in range(SPLITS):
                place = pl.multiple_of(begin % width + part * rows, rows)
                left = tok[begin // width, :, pl.ds(place, rows)]
                right = weights[first + part, source, :, :, pl.ds(at, tile)].reshape(rows, tile)
                term = jnp.dot(left, right, preferred_element_type=jnp.float32)
                total = term if total is None else total + term
        return total

    scale = 1.0 / jnp.sqrt(jnp.float32(HEAD))

    def resample(h):
        cols = pl.ds(h * HEAD, HEAD)
        scores = lax.dot_general(
            latent[:, cols], keys[:, cols], (((1,), (1,)), ((), ())), preferred_element_type=jnp.float32
        )
        update[:, cols] = jnp.dot(softmax_rows(scores * scale), tok[t, :, cols], preferred_element_type=jnp.float32)

    def carry(h):
        cols = pl.ds(h * HEAD, HEAD)

        @pl.when(s > 0)
        def _():
            remote(
                memory_out.at[:, cols], memory_in.at[:, cols], m_send.at[h], m_recv.at[h], {"seg": s - 1}
            ).wait_recv()

        memory_out[:, cols] = forget[:, cols] * memory_in[:, cols] + update[:, cols]

        @pl.when(s + 1 < segs)
        def _():
            m_copy(h).start()

    def readout(h):
        cols = pl.ds(h * HEAD, HEAD)
        held = memory_in[:, cols]
        normed = held * lax.rsqrt(jnp.mean(held * held, axis=-1, keepdims=True) + 1e-06)
        scores = lax.dot_general(
            queries[:, cols], normed.astype(jnp.bfloat16), (((1,), (1,)), ((), ())), preferred_element_type=jnp.float32
        )
        read = jnp.dot(softmax_rows(scores * scale), held.astype(jnp.bfloat16), preferred_element_type=jnp.float32)
        mixed[:, cols] = (tok[t, :, cols].astype(jnp.float32) + read).astype(jnp.bfloat16)

    def arrive_all_z(group, distance):
        for k in group:
            arrive_z(k, distance)

    def arrive_all_y(group, distance):
        for k in group:
            arrive_y(k, distance)

    for distance in range(1, vids):
        arrive_all_z(key_streams, distance)
        if distance == vids - 2:
            for k in query_streams:
                own_sends(k)
        if distance > 1:
            arrive_all_y(key_streams, distance - 1)
    arrive_all_y(key_streams, vids - 1)
    arrive_all_z(query_streams, 1)
    for distance in range(1, vids):
        for k in key_streams:
            arrive_d(k, distance)
    remote(tok.at[1 - t], tok.at[1 - t], tok_send, tok_recv, {"tp": 1 - t}).wait_recv()
    for at in range(0, width, tile):
        keys[:, pl.ds(at, tile)] = product(0, range(vids), at).astype(jnp.bfloat16)
    arrive_all_y(query_streams, 1)
    for h in range(heads // 2):
        resample(h)
    for distance in range(2, vids - 1):
        arrive_all_z(query_streams, distance)
    for h in range(heads // 2, heads):
        resample(h)

    @pl.when(s == 0)
    def _():
        first_memory.wait()

    @pl.when(y == 0)
    def _():
        for h in range(heads):
            carry(h)

    for distance in range(2, vids - 1):
        arrive_all_y(query_streams, distance)
    arrive_all_z(query_streams, vids - 1)
    for distance in range(1, vids - 1):
        for k in query_streams:
            arrive_d(k, distance, final=False)
    others = [(last + 1 + i) % vids for i in range(vids - 1)]
    for at in range(0, width, tile):
        partial[:, pl.ds(at, tile)] = product(SPLITS, others, at)

    @pl.when(y > 0)
    def _():
        for h in range(heads):
            carry(h)

    arrive_all_y(query_streams, vids - 1)
    for distance in range(1, vids):
        for k in query_streams:
            arrive_d(k, distance, final=True)
    per_tile = tile // HEAD
    for at in range(0, width, tile):
        cols = pl.ds(at, tile)
        queries[:, cols] = (partial[:, cols] + product(SPLITS, [last], at)).astype(jnp.bfloat16)
        for h in range(at // HEAD, at // HEAD + per_tile):
            readout(h)

    tok_copy.wait_send()
    for k in streams:
        for side in sides:
            @pl.when(inside(z + side, vids))
            def _(k=k, side=side):
                z_copy(k, z, side).wait_send()

        for distance in range(1, vids):
            def sent(source, side, k=k):
                @pl.when(inside(z + side, vids))
                def _():
                    z_copy(k, source, side).wait_send()

                for step in sides:
                    @pl.when(inside(y + step, chips))
                    def _(step=step):
                        y_copy(k, source, y, step).wait_send()

                d_copy(k, source, y, core).wait_send()

                def one(chip, step):
                    @pl.when(inside(y + step, chips))
                    def _():
                        y_copy(k, source, chip, step).wait_send()

                    d_copy(k, source, chip, core).wait_send()

                each_chip(one)

            each_source(distance, sent)

    @pl.when(s + 1 < segs)
    def _():
        for h in range(heads):
            m_copy(h).wait_send()


def fused_shards(sizes, tokens, key_weight, query_weight, latent_queries, init_memory, forget):
    segs, vids, tps = sizes
    local = tokens[0]
    count, width = local.shape
    latents = latent_queries.shape[0]
    rows = key_weight.shape[0]
    heads = width // HEAD
    chips = segs // CORES
    parts = (segs, rows // segs // SPLITS, width)
    streams = 2 * SPLITS
    anywhere = pl.BlockSpec(memory_space=pl.ANY)
    vmem = pl.BlockSpec(memory_space=pltpu.VMEM)
    dma = pltpu.SemaphoreType.DMA
    mixed, memory = pl.pallas_call(
        functools.partial(fused_kernel, segs, vids, tps),
        out_shape=(
            jax.ShapeDtypeStruct((count, width), jnp.bfloat16),
            jax.ShapeDtypeStruct((latents, width), jnp.float32),
        ),
        in_specs=[anywhere, anywhere, anywhere, vmem, anywhere, vmem],
        out_specs=(vmem, vmem),
        scratch_shapes=[
            pltpu.VMEM((streams, vids) + parts, jnp.bfloat16),
            pltpu.VMEM((tps, count, width), jnp.bfloat16),
            pltpu.VMEM((count, width), jnp.bfloat16),
            pltpu.VMEM((count, width), jnp.bfloat16),
            pltpu.VMEM((latents, width), jnp.float32),
            pltpu.VMEM((latents, width), jnp.float32),
            pltpu.VMEM((count, width), jnp.float32),
            dma((2 + streams,)),
            dma,
            dma,
            dma((streams, vids, 2)),
            dma((streams, vids)),
            dma((streams, vids, chips, 2)),
            dma((streams, vids, chips)),
            dma((streams, vids, chips)),
            dma((streams, vids, chips)),
            dma((heads,)),
            dma((heads,)),
        ],
        compiler_params=pltpu.CompilerParams(collective_id=0, has_side_effects=True),
    )(
        local,
        key_weight.reshape((SPLITS,) + parts),
        query_weight.reshape((SPLITS,) + parts),
        latent_queries,
        init_memory[0],
        forget[0],
    )
    return (mixed[None], memory[None])


def relay_fits(segs, vids, tps):
    return tps == 2 and segs % CORES == 0 and vids > 2 and segs * vids <= 32


def solution(mesh):
    placed = (
        P("vid", "seg", "tp"),
        P("vid", "tp"),
        P("vid", "tp"),
        P(None, "tp"),
        P("vid", None, "tp"),
        P("vid", "seg", "tp"),
    )
    sizes = tuple(mesh.shape[axis] for axis in ("seg", "vid", "tp"))
    body = functools.partial(fused_shards, sizes) if relay_fits(*sizes) else shards
    return jax.shard_map(
        body,
        mesh=mesh,
        in_specs=placed,
        out_specs=(P("vid", "seg", "tp"), P("vid", "seg", "tp")),
        check_vma=False,
    )
```

profile of v0, /device:TPU:4, one launch (start us, length us, event | category | flops | bytes accessed | tf_op | source)
XLA Modules:
  0.0 64.0 jit_solution(14827951164756083901)
XLA Ops:
  0.6 60.2 %shard_map.77 = (bf16[512,1024]{1,0:T(8,128)(2,1)}, f32[128,1024]{1,0:T(8,128)}) custom-call(bf16[512,1024]{1,0:T(8,128)(2,1)} %bitcast.7, bf16[2,4,64,1024]{3,2,1,0:T(8,128)(2,1)} %bitcast.8, bf16[2,4,64,1024]{3,2,1,0:T(8,128)(2,1)} %bitcast.9, bf16[128,1024]{1,0:T(8,128)(2,1)} %latent.1, f32[128,1024]{1,0:T(8,128)} %bitcast.11, f32[1,1024]{1,0:T(1,128)} %bitcast.13), custom_call_target="tpu_custom_call" | custom-call | tf_op jit(solution)/shard_map/pallas_call | solution.py:415
  60.9 0.0 copy-start
  60.9 2.3 %copy.10 = bf16[1,512,1024]{2,1,0:T(8,128)(2,1)} copy(bf16[1,512,1024]{2,1,0:T(8,128)(2,1)} %bitcast.10) | data formatting | bytes 2097152
  63.2 0.0 copy-done
  63.2 0.8 %copy.11 = f32[1,128,1024]{2,1,0:T(8,128)} copy(f32[1,128,1024]{2,1,0:T(8,128)S(1)} %bitcast.12) | data formatting | bytes 1048576
Async XLA Ops:
  60.9 2.3 %copy-start = (f32[128,1024]{1,0:T(8,128)S(1)}, f32[128,1024]{1,0:T(8,128)}, u32[]{:S(2)}) copy-start(f32[128,1024]{1,0:T(8,128)} %get-tuple-element.5) | copy-start | bytes 1572868
where the time goes:
time: 64.2 us; the launch traced here: 64 us
  Pallas kernels  60.2 us (94%)
  local copies, waits for them, and re-layouts  3.12 us (5%)
  between operations  0.65 us (1%)
    pallas_call x1, Pallas kernels, fused_shards(): pl.pallas_call(functools.partial(fused_kernel, segs, vids, tps), out_shap...  60.2 us
    unnamed x4, local copies, waits for them, and re-layouts  3.12 us

commit v1 on v0

v1 whole, which is shorter than its diff:
```python
import functools

import jax
import jax.numpy as jnp
from jax import lax
from jax.experimental import pallas as pl
from jax.experimental.pallas import tpu as pltpu
from jax.sharding import PartitionSpec as P

HEAD = 128


def from_behind(block, axis, distance):
    devices = range(lax.axis_size(axis))
    route = [(i - distance, i) for i in devices if i - distance in devices]
    return lax.ppermute(block, axis, route)


def trailing_softmax(scores):
    top = jnp.max(scores, axis=-1, keepdims=True)
    expo = jnp.exp(scores - top)
    return expo / jnp.sum(expo, axis=-1, keepdims=True)


def add_rows(left, piece):
    return jnp.dot(left, piece, preferred_element_type=jnp.float32)


def shards(tokens, key_weight, query_weight, latent_queries, init_memory, forget):
    local = tokens[0]
    width = local.shape[1]
    heads = width // HEAD
    latents = latent_queries.shape[0]
    whole = lax.all_gather(local, "tp", axis=1, tiled=True)

    def add_one(piece):
        return add_rows(whole, piece)

    keys_full = add_one(lax.all_gather(key_weight, "vid", axis=0, tiled=True))
    queries_full = add_one(lax.all_gather(query_weight, "vid", axis=0, tiled=True))
    scale = 1.0 / jnp.sqrt(jnp.float32(HEAD))
    keys = keys_full.astype(jnp.bfloat16).reshape(-1, heads, HEAD)
    queries = queries_full.astype(jnp.bfloat16).reshape(-1, heads, HEAD)
    values = local.reshape(-1, heads, HEAD)
    latent = latent_queries.reshape(latents, heads, HEAD)
    scores = jnp.einsum("mhe,the->hmt", latent, keys, preferred_element_type=jnp.float32) * scale
    weight_params = trailing_softmax(scores).astype(jnp.bfloat16)
    update = jnp.einsum(
        "hmt,the->mhe", weight_params, values, preferred_element_type=jnp.float32
    ).reshape(latents, width)
    retain = forget[0]
    initial_memory = init_memory[0]
    first = lax.axis_index("seg") == 0

    def turn(step, memory_now):
        received = from_behind(retain * memory_now + update, "seg", 1)
        return jnp.where(first, initial_memory, received)

    memory_in = lax.fori_loop(0, lax.axis_size("seg") - 1, turn, initial_memory)
    memory_out = retain * memory_in + update
    grouped = memory_in.reshape(latents, heads, HEAD)
    normed = grouped * lax.rsqrt(jnp.mean(grouped * grouped, axis=-1, keepdims=True) + 1e-06)
    read_scores = (
        jnp.einsum(
            "the,mhe->htm", queries, normed.astype(jnp.bfloat16), preferred_element_type=jnp.float32
        )
        * scale
    )
    read_weights = trailing_softmax(read_scores).astype(jnp.bfloat16)
    read = jnp.einsum(
        "htm,mhe->the",
        read_weights,
        grouped.astype(jnp.bfloat16),
        preferred_element_type=jnp.float32,
    )
    mixed = (local.astype(jnp.float32) + read.reshape(-1, width)).astype(jnp.bfloat16)
    return (mixed[None], memory_out[None])


CORES = 2
TILE = 2 * HEAD
AHEAD = 4
BEHIND = 2


def softmax_rows(scores):
    top = jnp.max(scores, axis=-1, keepdims=True)
    expo = jnp.exp(scores - top)
    return (expo * (1.0 / jnp.sum(expo, axis=-1, keepdims=True))).astype(jnp.bfloat16)


def fused_kernel(
    segs, vids, tps,
    tokens, key_w, query_w, latent_in, init_memory, forget_in,
    mixed, memory_out,
    weights, tok, queries, memory_in, update, partial, latent, forget,
    load_sem, tok_send, tok_recv, z_send, z_recv, y_send, y_recv, d_send, d_recv, m_send, m_recv,
):
    s, z, t = lax.axis_index("seg"), lax.axis_index("vid"), lax.axis_index("tp")
    y, core = s // CORES, s % CORES
    partner = y * CORES + (1 - core)
    across = (1 - y) * CORES + core
    count, width = tokens.shape
    tiles = width // TILE
    blocks = vids // tps
    depth = blocks * weights.shape[2] * weights.shape[3]
    chunks = range(2 * tiles)
    sides = (1, -1)

    def remote(src, dst, send, recv, device):
        return pltpu.make_async_remote_copy(
            src_ref=src, dst_ref=dst, send_sem=send, recv_sem=recv,
            device_id=device, device_id_type=pl.DeviceIdType.MESH,
        )

    def tile_cols(k):
        return pl.ds(k % tiles * TILE, TILE)

    def z_copy(k, source, side):
        block = weights.at[k, source, s]
        return remote(block, block, z_send.at[k, source, (1 - side) // 2], z_recv.at[k, source], {"vid": z + side})

    def y_copy(k, source, owner):
        block = weights.at[k, source, owner]
        return remote(block, block, y_send.at[k, source], y_recv.at[k, source], {"seg": across})

    def d_copy(k, source, owner, kind):
        block = weights.at[k, source, owner]
        return remote(block, block, d_send.at[k, source, kind], d_recv.at[k, source, kind], {"seg": partner})

    def m_copy(c, device):
        cols = tile_cols(c)
        return remote(memory_out.at[:, cols], memory_in.at[:, cols], m_send.at[c], m_recv.at[c], {"seg": device})

    def inside(index, size):
        return (index >= 0) & (index < size)

    def flag(condition):
        return jnp.where(condition, 1, 0).astype(jnp.int32)

    loads = [
        pltpu.make_async_copy(
            (key_w, query_w)[k // tiles].at[:, :, tile_cols(k)], weights.at[k, z], load_sem.at[k]
        )
        for k in chunks
    ]
    tok_load = pltpu.make_async_copy(tokens, tok.at[t], load_sem.at[len(loads)])
    first_memory = pltpu.make_async_copy(init_memory, memory_in, load_sem.at[len(loads) + 1])
    latent_load = pltpu.make_async_copy(latent_in, latent, load_sem.at[len(loads) + 2])
    forget_load = pltpu.make_async_copy(forget_in, forget, load_sem.at[len(loads) + 3])
    for load in loads[:1] + [tok_load] + loads[1:] + [latent_load, forget_load]:
        load.start()

    @pl.when(s == 0)
    def _():
        first_memory.start()

    barrier = pltpu.get_barrier_semaphore()
    greeted = [
        (z + 1 < vids, {"vid": z + 1}),
        (z > 0, {"vid": z - 1}),
        (s >= 0, {"seg": across}),
        ((core == 1) & (y == 0), {"seg": s + 1}),
        ((core == 0) & (y == 1), {"seg": s - 1}),
        (s >= 0, {"seg": partner}),
        (s >= 0, {"tp": 1 - t}),
    ]
    waited = 0
    for condition, device in greeted:
        waited = waited + flag(condition)

        @pl.when(condition)
        def _(device=device):
            pl.semaphore_signal(barrier, inc=1, device_id=device, device_id_type=pl.DeviceIdType.MESH)

    pl.semaphore_wait(barrier, waited)

    def own_sends(k):
        for side in sides:
            @pl.when(inside(z + side, vids))
            def _(side=side):
                z_copy(k, z, side).start()

    tok_copy = remote(tok.at[t], tok.at[t], tok_send, tok_recv, {"tp": 1 - t})
    for k in chunks[:AHEAD]:
        loads[k].wait()
        own_sends(k)
        if k == 0:
            tok_load.wait()
            tok_copy.start()
    for k in chunks[AHEAD:]:
        loads[k].wait()
    latent_load.wait()
    forget_load.wait()

    @pl.when(s == 0)
    def _():
        first_memory.wait()

    def each_source(distance, action):
        for side in sides:
            source = z - side * distance

            @pl.when(inside(source, vids))
            def _(source=source, side=side):
                action(source, side)

    def arrive_z(k, distance):
        def action(source, side):
            z_copy(k, source, side).wait_recv()

            @pl.when(inside(z + side, vids))
            def _():
                z_copy(k, source, side).start()

            y_copy(k, source, s).start()
            d_copy(k, source, s, 0).start()

        each_source(distance, action)
        if distance == vids - 1 and k + AHEAD < len(chunks):
            own_sends(k + AHEAD)

    def arrive_y(k, distance):
        def action(source, side):
            y_copy(k, source, across).wait_recv()
            d_copy(k, source, across, 1).start()

        each_source(distance, action)

    def arrive_d(k):
        for distance in range(1, vids):
            def action(source, side):
                d_copy(k, source, partner, 0).wait_recv()
                d_copy(k, source, (1 - y) * CORES + 1 - core, 1).wait_recv()

            each_source(distance, action)

    def half_product(k, half):
        right = weights[k, pl.ds(half * blocks, blocks)].reshape(depth, TILE)
        return jnp.dot(tok[half], right, preferred_element_type=jnp.float32)

    scale = 1.0 / jnp.sqrt(jnp.float32(HEAD))

    def key_near(k):
        arrive_d(k)
        partial[k] = half_product(k, t)

    def key_far(k):
        keys = (partial[k] + half_product(k, 1 - t)).astype(jnp.bfloat16)
        for h in range(TILE // HEAD):
            cols = pl.ds(k * TILE + h * HEAD, HEAD)
            scores = lax.dot_general(
                latent[:, cols], keys[:, h * HEAD:(h + 1) * HEAD], (((1,), (1,)), ((), ())),
                preferred_element_type=jnp.float32,
            )
            update[:, cols] = jnp.dot(softmax_rows(scores * scale), tok[t, :, cols], preferred_element_type=jnp.float32)

    def carry(c, seg):
        cols = tile_cols(c)

        @pl.when(s == seg)
        def _():
            if seg > 0:
                m_copy(c, s - 1).wait_recv()
            memory_out[:, cols] = forget[:, cols] * memory_in[:, cols] + update[:, cols]
            if seg + 1 < segs:
                m_copy(c, s + 1).start()

    def query(k):
        arrive_d(k)
        queries[:, tile_cols(k)] = (half_product(k, t) + half_product(k, 1 - t)).astype(jnp.bfloat16)

    def readout(k):
        for h in range(TILE // HEAD):
            cols = pl.ds(k % tiles * TILE + h * HEAD, HEAD)
            held = memory_in[:, cols]
            normed = held * lax.rsqrt(jnp.mean(held * held, axis=-1, keepdims=True) + 1e-06)
            scores = lax.dot_general(
                queries[:, cols], normed.astype(jnp.bfloat16), (((1,), (1,)), ((), ())),
                preferred_element_type=jnp.float32,
            )
            read = jnp.dot(softmax_rows(scores * scale), held.astype(jnp.bfloat16), preferred_element_type=jnp.float32)
            mixed[:, cols] = (tok[t, :, cols].astype(jnp.float32) + read).astype(jnp.bfloat16)

    def far_tokens():
        remote(tok.at[1 - t], tok.at[1 - t], tok_send, tok_recv, {"tp": 1 - t}).wait_recv()

    gaps = vids - 1
    slots = [(k, distance) for k in chunks for distance in range(1, vids)]
    tasks = {}

    def place(slot, task, *args):
        tasks.setdefault(min(slot, len(slots) + BEHIND), []).append((task, args))

    done = [gaps * k + gaps - 1 + BEHIND + 1 for k in chunks]
    for k in range(tiles):
        place(done[k], key_near, k)
    start = done[tiles - 1]
    place(start, far_tokens)
    for k in range(tiles):
        place(start + k, key_far, k)
        for seg, lag in enumerate((0, 1, 4, 5)):
            place(start + k + lag, carry, k, seg)
    for k in range(tiles, 2 * tiles):
        place(done[k], query, k)
    for k in range(tiles, 2 * tiles):
        place(max(done[k], start + k - tiles + 6), readout, k)

    for at in range(len(slots) + BEHIND + 1):
        if at < len(slots):
            arrive_z(*slots[at])
        if 0 <= at - BEHIND < len(slots):
            arrive_y(*slots[at - BEHIND])
        for task, args in tasks.get(at, []):
            task(*args)

    tok_copy.wait_send()
    for k in chunks:
        for side in sides:
            @pl.when(inside(z + side, vids))
            def _(k=k, side=side):
                z_copy(k, z, side).wait_send()

        for distance in range(1, vids):
            def sent(source, side, k=k):
                @pl.when(inside(z + side, vids))
                def _():
                    z_copy(k, source, side).wait_send()

                y_copy(k, source, s).wait_send()
                d_copy(k, source, s, 0).wait_send()
                d_copy(k, source, across, 1).wait_send()

            each_source(distance, sent)

    @pl.when(s + 1 < segs)
    def _():
        for c in range(tiles):
            m_copy(c, s + 1).wait_send()


def fused_shards(sizes, tokens, key_weight, query_weight, latent_queries, init_memory, forget):
    segs, vids, tps = sizes
    local = tokens[0]
    count, width = local.shape
    latents = latent_queries.shape[0]
    rows = key_weight.shape[0]
    tiles = width // TILE
    parts = (segs, rows // segs, width)
    hbm = pl.BlockSpec(memory_space=pltpu.HBM)
    vmem = pl.BlockSpec(memory_space=pltpu.VMEM)
    dma = pltpu.SemaphoreType.DMA
    mixed, memory = pl.pallas_call(
        functools.partial(fused_kernel, segs, vids, tps),
        out_shape=(
            jax.ShapeDtypeStruct((count, width), jnp.bfloat16),
            jax.ShapeDtypeStruct((latents, width), jnp.float32),
        ),
        in_specs=[hbm] * 6,
        out_specs=(vmem, vmem),
        scratch_shapes=[
            pltpu.VMEM((2 * tiles, vids, segs, rows // segs, TILE), jnp.bfloat16),
            pltpu.VMEM((tps, count, width), jnp.bfloat16),
            pltpu.VMEM((count, width), jnp.bfloat16),
            pltpu.VMEM((latents, width), jnp.float32),
            pltpu.VMEM((latents, width), jnp.float32),
            pltpu.VMEM((tiles, count, TILE), jnp.float32),
            pltpu.VMEM((latents, width), jnp.bfloat16),
            pltpu.VMEM((1, width), jnp.float32),
            dma((2 * tiles + 4,)),
            dma,
            dma,
            dma((2 * tiles, vids, 2)),
            dma((2 * tiles, vids)),
            dma((2 * tiles, vids)),
            dma((2 * tiles, vids)),
            dma((2 * tiles, vids, 2)),
            dma((2 * tiles, vids, 2)),
            dma((tiles,)),
            dma((tiles,)),
        ],
        compiler_params=pltpu.CompilerParams(
            collective_id=0, has_side_effects=True, vmem_limit_bytes=GRANT
        ),
    )(
        *(
            pltpu.with_memory_space_constraint(array, pltpu.HBM)
            for array in (
                local, key_weight.reshape(parts), query_weight.reshape(parts), latent_queries, init_memory[0], forget[0]
            )
        )
    )
    return (mixed[None], memory[None])


GRANT = 28 * 1024 * 1024


def relay_fits(segs, vids, tps):
    return tps == 2 and segs == 2 * CORES and vids > 2 and vids % tps == 0 and segs * vids <= 32


def solution(mesh):
    placed = (
        P("vid", "seg", "tp"),
        P("vid", "tp"),
        P("vid", "tp"),
        P(None, "tp"),
        P("vid", None, "tp"),
        P("vid", "seg", "tp"),
    )
    sizes = tuple(mesh.shape[axis] for axis in ("seg", "vid", "tp"))
    body = functools.partial(fused_shards, sizes) if relay_fits(*sizes) else shards
    return jax.shard_map(
        body,
        mesh=mesh,
        in_specs=placed,
        out_specs=(P("vid", "seg", "tp"), P("vid", "seg", "tp")),
        check_vma=False,
    )
```

time: 64.2 us -> 70.2 us (1.093)
  the two profiles are of different devices: /device:TPU:4 before, /device:TPU:0 now
where the time goes in v1:
time: 70.2 us; the launch traced here: 69.3 us
  Pallas kernels  66.9 us (95%)
  local copies, waits for them, and re-layouts  1.77 us (3%)
    pallas_call x1, Pallas kernels, fused_shards(): pl.pallas_call(functools.partial(fused_kernel, segs, vids, tps), out_shap...  66.9 us
    unnamed x2, local copies, waits for them, and re-layouts  1.77 us

profile of v1, /device:TPU:0, one launch (start us, length us, event | category | flops | bytes accessed | tf_op | source)
XLA Modules:
  0.0 69.3 jit_solution(16922357728859290877)
XLA Ops:
  0.6 66.9 %shard_map.77 = (bf16[512,1024]{1,0:T(8,128)(2,1)S(1)}, f32[128,1024]{1,0:T(8,128)S(1)}) custom-call(bf16[512,1024]{1,0:T(8,128)(2,1)} %bitcast.9, bf16[4,128,1024]{2,1,0:T(8,128)(2,1)} %bitcast.10, bf16[4,128,1024]{2,1,0:T(8,128)(2,1)} %bitcast.11, bf16[128,1024]{1,0:T(8,128)(2,1)} %latent_in.1, f32[128,1024]{1,0:T(8,128)} %bitcast.12, f32[1,1024]{1,0:T(1,128)} %bitcast.13), custom_call_target="tpu_custom_call" | custom-call | tf_op jit(solution)/shard_map/pallas_call | solution.py:353
  67.5 1.0 %copy.10 = bf16[1,512,1024]{2,1,0:T(8,128)(2,1)} copy(bf16[1,512,1024]{2,1,0:T(8,128)(2,1)S(1)} %bitcast.7) | data formatting | bytes 2097152
  68.5 0.8 %copy.11 = f32[1,128,1024]{2,1,0:T(8,128)} copy(f32[1,128,1024]{2,1,0:T(8,128)S(1)} %bitcast.8) | data formatting | bytes 1048576

commit v2 on v1

--- a/solution.py
+++ b/solution.py
@@ -79,8 +79,16 @@
 
 CORES = 2
 TILE = 2 * HEAD
-AHEAD = 4
-BEHIND = 2
+AHEAD = 3
+SKEW = 1
+HOLD = 0
+BEHIND = 4
+LATE = 4
+DIRECT = 1
+EARLY = 1
+STEP = 0
+LAGS = (0, 1, 8, 9)
+GROUP = 4
 
 
 def softmax_rows(scores):
@@ -93,7 +101,7 @@
     segs, vids, tps,
     tokens, key_w, query_w, latent_in, init_memory, forget_in,
     mixed, memory_out,
-    weights, tok, queries, memory_in, update, partial, latent, forget,
+    weights, tok, queries, memory_in, update, partial, raised, flipped, latent, forget,
     load_sem, tok_send, tok_recv, z_send, z_recv, y_send, y_recv, d_send, d_recv, m_send, m_recv,
 ):
     s, z, t = lax.axis_index("seg"), lax.axis_index("vid"), lax.axis_index("tp")
@@ -116,9 +124,14 @@
     def tile_cols(k):
         return pl.ds(k % tiles * TILE, TILE)
 
-    def z_copy(k, source, side):
-        block = weights.at[k, source, s]
-        return remote(block, block, z_send.at[k, source, (1 - side) // 2], z_recv.at[k, source], {"vid": z + side})
+    def lanes(k):
+        return (s, across) if k >= len(chunks) - DIRECT else (s,)
+
+    def z_copy(k, source, side, lane):
+        block = weights.at[k, source, lanes(k)[lane]]
+        return remote(
+            block, block, z_send.at[k, source, (1 - side) // 2, lane], z_recv.at[k, source, lane], {"vid": z + side}
+        )
 
     def y_copy(k, source, owner):
         block = weights.at[k, source, owner]
@@ -179,7 +192,8 @@
         for side in sides:
             @pl.when(inside(z + side, vids))
             def _(side=side):
-                z_copy(k, z, side).start()
+                for lane in range(len(lanes(k))):
+                    z_copy(k, z, side, lane).start()
 
     tok_copy = remote(tok.at[t], tok.at[t], tok_send, tok_recv, {"tp": 1 - t})
     for k in chunks[:AHEAD]:
@@ -207,17 +221,19 @@
 
     def arrive_z(k, distance):
         def action(source, side):
-            z_copy(k, source, side).wait_recv()
-
-            @pl.when(inside(z + side, vids))
-            def _():
-                z_copy(k, source, side).start()
-
-            y_copy(k, source, s).start()
-            d_copy(k, source, s, 0).start()
+            for lane, owner in enumerate(lanes(k)):
+                z_copy(k, source, side, lane).wait_recv()
+
+                @pl.when(inside(z + side, vids))
+                def _(lane=lane):
+                    z_copy(k, source, side, lane).start()
+
+                if len(lanes(k)) == 1:
+                    y_copy(k, source, owner).start()
+                d_copy(k, source, owner, lane).start()
 
         each_source(distance, action)
-        if distance == vids - 1 and k + AHEAD < len(chunks):
+        if distance == 1 and k + AHEAD < len(chunks):
             own_sends(k + AHEAD)
 
     def arrive_y(k, distance):
@@ -225,7 +241,8 @@
             y_copy(k, source, across).wait_recv()
             d_copy(k, source, across, 1).start()
 
-        each_source(distance, action)
+        if len(lanes(k)) == 1:
+            each_source(distance, action)
 
     def arrive_d(k):
         for distance in range(1, vids):
@@ -241,6 +258,9 @@
 
     scale = 1.0 / jnp.sqrt(jnp.float32(HEAD))
 
+    def flip(k):
+        flipped[tile_cols(k)] = tok[t, :, tile_cols(k)].T
+
     def key_near(k):
         arrive_d(k)
         partial[k] = half_product(k, t)
@@ -249,11 +269,22 @@
         keys = (partial[k] + half_product(k, 1 - t)).astype(jnp.bfloat16)
         for h in range(TILE // HEAD):
             cols = pl.ds(k * TILE + h * HEAD, HEAD)
-            scores = lax.dot_general(
-                latent[:, cols], keys[:, h * HEAD:(h + 1) * HEAD], (((1,), (1,)), ((), ())),
+            raised[:, cols] = lax.dot_general(
+                keys[:, h * HEAD:(h + 1) * HEAD], latent[:, cols], (((1,), (1,)), ((), ())),
                 preferred_element_type=jnp.float32,
-            )
-            update[:, cols] = jnp.dot(softmax_rows(scores * scale), tok[t, :, cols], preferred_element_type=jnp.float32)
+            ) * scale
+
+    def blend(group):
+        at = group[0] * TILE
+        span = len(group) * TILE
+        scores = raised[:, at:at + span]
+        expo = jnp.exp(scores - jnp.max(scores, axis=0, keepdims=True))
+        held = (expo * (1.0 / jnp.sum(expo, axis=0, keepdims=True))).astype(jnp.bfloat16)
+        for h in range(span // HEAD):
+            cols = pl.ds(at + h * HEAD, HEAD)
+            update[:, cols] = jnp.dot(
+                flipped[cols], held[:, h * HEAD:(h + 1) * HEAD], preferred_element_type=jnp.float32
+            ).T
 
     def carry(c, seg):
         cols = tile_cols(c)
@@ -287,47 +318,58 @@
 
     gaps = vids - 1
     slots = [(k, distance) for k in chunks for distance in range(1, vids)]
-    tasks = {}
-
-    def place(slot, task, *args):
-        tasks.setdefault(min(slot, len(slots) + BEHIND), []).append((task, args))
-
-    done = [gaps * k + gaps - 1 + BEHIND + 1 for k in chunks]
+    slots.sort(key=lambda slot: (slot[0] + SKEW * (slot[1] - 1) + HOLD * (slot[0] >= tiles), slot[1]))
+    relays = [
+        (at + (BEHIND if slot[0] < tiles else LATE), slot) for at, slot in enumerate(slots) if len(lanes(slot[0])) == 1
+    ]
+    done = {k: slots.index((k, gaps)) + 1 for k in chunks}
+    for at, (k, _) in relays:
+        done[k] = max(done[k], at + 1)
+    plan = []
+
+    def place(at, task, *args):
+        plan.append((at, task, args))
+
+    start = done[tiles - 1] - EARLY
     for k in range(tiles):
+        place(k + 1, flip, k)
         place(done[k], key_near, k)
-    start = done[tiles - 1]
     place(start, far_tokens)
     for k in range(tiles):
-        place(start + k, key_far, k)
-        for seg, lag in enumerate((0, 1, 4, 5)):
-            place(start + k + lag, carry, k, seg)
+        place(max(start, done[k]) + STEP * k, key_far, k)
+    mixed_at = max(start, done[tiles - 1]) + STEP * (tiles - 1)
+    for at in range(0, tiles, GROUP):
+        place(mixed_at, blend, range(at, min(at + GROUP, tiles)))
+    for k in range(tiles):
+        for seg, lag in enumerate(LAGS):
+            place(mixed_at + lag, carry, k, seg)
     for k in range(tiles, 2 * tiles):
         place(done[k], query, k)
-    for k in range(tiles, 2 * tiles):
-        place(max(done[k], start + k - tiles + 6), readout, k)
-
-    for at in range(len(slots) + BEHIND + 1):
-        if at < len(slots):
-            arrive_z(*slots[at])
-        if 0 <= at - BEHIND < len(slots):
-            arrive_y(*slots[at - BEHIND])
-        for task, args in tasks.get(at, []):
-            task(*args)
+        place(max(done[k], mixed_at + LAGS[-1]), readout, k)
+    for at, slot in enumerate(slots):
+        place(at - 0.2, arrive_z, *slot)
+    for at, slot in relays:
+        place(at - 0.1, arrive_y, *slot)
+    for at, task, args in sorted(plan, key=lambda entry: entry[0]):
+        task(*args)
 
     tok_copy.wait_send()
     for k in chunks:
         for side in sides:
             @pl.when(inside(z + side, vids))
             def _(k=k, side=side):
-                z_copy(k, z, side).wait_send()
+                for lane in range(len(lanes(k))):
+                    z_copy(k, z, side, lane).wait_send()
 
         for distance in range(1, vids):
             def sent(source, side, k=k):
                 @pl.when(inside(z + side, vids))
                 def _():
-                    z_copy(k, source, side).wait_send()
-
-                y_copy(k, source, s).wait_send()
+                    for lane in range(len(lanes(k))):
+                        z_copy(k, source, side, lane).wait_send()
+
+                if len(lanes(k)) == 1:
+                    y_copy(k, source, s).wait_send()
                 d_copy(k, source, s, 0).wait_send()
                 d_copy(k, source, across, 1).wait_send()
 
@@ -365,13 +407,15 @@
             pltpu.VMEM((latents, width), jnp.float32),
             pltpu.VMEM((latents, width), jnp.float32),
             pltpu.VMEM((tiles, count, TILE), jnp.float32),
+            pltpu.VMEM((count, width), jnp.float32),
+            pltpu.VMEM((width, count), jnp.bfloat16),
             pltpu.VMEM((latents, width), jnp.bfloat16),
             pltpu.VMEM((1, width), jnp.float32),
             dma((2 * tiles + 4,)),
             dma,
             dma,
+            dma((2 * tiles, vids, 2, 2)),
             dma((2 * tiles, vids, 2)),
-            dma((2 * tiles, vids)),
             dma((2 * tiles, vids)),
             dma((2 * tiles, vids)),
             dma((2 * tiles, vids, 2)),

time: 70.2 us -> 58 us (0.83)
  Pallas kernels: 66.9 us -> 55.2 us
    pallas_call x1, Pallas kernels: 66.9 us -> 55.2 us  [fused_shards(): pl.pallas_call(functools.partial(fused_kernel, segs, vids, tps), out_shap...]
where the time goes in v2:
time: 58 us; the launch traced here: 57.6 us
  Pallas kernels  55.2 us (95%)
  local copies, waits for them, and re-layouts  1.77 us (3%)
  between operations  0.64 us (1%)
    pallas_call x1, Pallas kernels, fused_shards(): pl.pallas_call(functools.partial(fused_kernel, segs, vids, tps), out_shap...  55.2 us
    unnamed x2, local copies, waits for them, and re-layouts  1.77 us

profile of v2, /device:TPU:0, one launch (start us, length us, event | category | flops | bytes accessed | tf_op | source)
XLA Modules:
  0.0 57.6 jit_solution(9620304466785058636)
XLA Ops:
  0.6 55.2 %shard_map.77 = (bf16[512,1024]{1,0:T(8,128)(2,1)S(1)}, f32[128,1024]{1,0:T(8,128)S(1)}) custom-call(bf16[512,1024]{1,0:T(8,128)(2,1)} %bitcast.9, bf16[4,128,1024]{2,1,0:T(8,128)(2,1)} %bitcast.10, bf16[4,128,1024]{2,1,0:T(8,128)(2,1)} %bitcast.11, bf16[128,1024]{1,0:T(8,128)(2,1)} %latent_in.1, f32[128,1024]{1,0:T(8,128)} %bitcast.12, f32[1,1024]{1,0:T(1,128)} %bitcast.13), custom_call_target="tpu_custom_call" | custom-call | tf_op jit(solution)/shard_map/pallas_call | solution.py:395
  55.9 1.0 %copy.10 = bf16[1,512,1024]{2,1,0:T(8,128)(2,1)} copy(bf16[1,512,1024]{2,1,0:T(8,128)(2,1)S(1)} %bitcast.7) | data formatting | bytes 2097152
  56.8 0.8 %copy.11 = f32[1,128,1024]{2,1,0:T(8,128)} copy(f32[1,128,1024]{2,1,0:T(8,128)S(1)} %bitcast.8) | data formatting | bytes 1048576

commit v3 on v2

--- a/solution.py
+++ b/solution.py
@@ -84,10 +84,10 @@
 HOLD = 0
 BEHIND = 4
 LATE = 4
-DIRECT = 1
+DIRECT = 2
 EARLY = 1
 STEP = 0
-LAGS = (0, 1, 8, 9)
+LAGS = (0, 1, 6, 7)
 GROUP = 4
 
 
@@ -133,6 +133,9 @@
             block, block, z_send.at[k, source, (1 - side) // 2, lane], z_recv.at[k, source, lane], {"vid": z + side}
         )
 
+    def through(source, side):
+        return (vids - 1 - source if side == 1 else source) > 1
+
     def y_copy(k, source, owner):
         block = weights.at[k, source, owner]
         return remote(block, block, y_send.at[k, source], y_recv.at[k, source], {"seg": across})
@@ -192,8 +195,12 @@
         for side in sides:
             @pl.when(inside(z + side, vids))
             def _(side=side):
-                for lane in range(len(lanes(k))):
-                    z_copy(k, z, side, lane).start()
+                z_copy(k, z, side, 0).start()
+
+            if len(lanes(k)) > 1:
+                @pl.when(inside(z + side, vids) & through(z, side))
+                def _(side=side):
+                    z_copy(k, z, side, 1).start()
 
     tok_copy = remote(tok.at[t], tok.at[t], tok_send, tok_recv, {"tp": 1 - t})
     for k in chunks[:AHEAD]:
@@ -221,16 +228,28 @@
 
     def arrive_z(k, distance):
         def action(source, side):
-            for lane, owner in enumerate(lanes(k)):
+            def take(lane):
                 z_copy(k, source, side, lane).wait_recv()
 
                 @pl.when(inside(z + side, vids))
-                def _(lane=lane):
+                def _():
                     z_copy(k, source, side, lane).start()
 
-                if len(lanes(k)) == 1:
-                    y_copy(k, source, owner).start()
-                d_copy(k, source, owner, lane).start()
+                d_copy(k, source, (s, across)[lane], lane).start()
+
+            take(0)
+            if len(lanes(k)) == 1:
+                y_copy(k, source, s).start()
+            elif distance > 1:
+                take(1)
+            else:
+                @pl.when(through(source, side))
+                def _():
+                    take(1)
+
+                @pl.when(jnp.logical_not(through(source, side)))
+                def _():
+                    y_copy(k, source, s).start()
 
         each_source(distance, action)
         if distance == 1 and k + AHEAD < len(chunks):
@@ -238,11 +257,16 @@
 
     def arrive_y(k, distance):
         def action(source, side):
-            y_copy(k, source, across).wait_recv()
-            d_copy(k, source, across, 1).start()
-
-        if len(lanes(k)) == 1:
-            each_source(distance, action)
+            def take():
+                y_copy(k, source, across).wait_recv()
+                d_copy(k, source, across, 1).start()
+
+            if len(lanes(k)) == 1:
+                take()
+            else:
+                pl.when(jnp.logical_not(through(source, side)))(take)
+
+        each_source(distance, action)
 
     def arrive_d(k):
         for distance in range(1, vids):
@@ -320,7 +344,8 @@
     slots = [(k, distance) for k in chunks for distance in range(1, vids)]
     slots.sort(key=lambda slot: (slot[0] + SKEW * (slot[1] - 1) + HOLD * (slot[0] >= tiles), slot[1]))
     relays = [
-        (at + (BEHIND if slot[0] < tiles else LATE), slot) for at, slot in enumerate(slots) if len(lanes(slot[0])) == 1
+        (at + (BEHIND if slot[0] < tiles else LATE), slot) for at, slot in enumerate(slots)
+        if len(lanes(slot[0])) == 1 or slot[1] == 1
     ]
     done = {k: slots.index((k, gaps)) + 1 for k in chunks}
     for at, (k, _) in relays:
@@ -358,8 +383,12 @@
         for side in sides:
             @pl.when(inside(z + side, vids))
             def _(k=k, side=side):
-                for lane in range(len(lanes(k))):
-                    z_copy(k, z, side, lane).wait_send()
+                z_copy(k, z, side, 0).wait_send()
+
+            if len(lanes(k)) > 1:
+                @pl.when(inside(z + side, vids) & through(z, side))
+                def _(k=k, side=side):
+                    z_copy(k, z, side, 1).wait_send()
 
         for distance in range(1, vids):
             def sent(source, side, k=k):
@@ -370,6 +399,11 @@
 
                 if len(lanes(k)) == 1:
                     y_copy(k, source, s).wait_send()
+                elif distance == 1:
+                    @pl.when(jnp.logical_not(through(source, side)))
+                    def _():
+                        y_copy(k, source, s).wait_send()
+
                 d_copy(k, source, s, 0).wait_send()
                 d_copy(k, source, across, 1).wait_send()
 

time: 58 us -> 57.1 us (0.984)
  Pallas kernels: 55.2 us -> 54.5 us
    pallas_call x1, Pallas kernels: 55.2 us -> 54.5 us  [fused_shards(): pl.pallas_call(functools.partial(fused_kernel, segs, vids, tps), out_shap...]
where the time goes in v3:
time: 57.1 us; the launch traced here: 56.9 us
  Pallas kernels  54.5 us (95%)
  local copies, waits for them, and re-layouts  1.77 us (3%)
  between operations  0.64 us (1%)
    pallas_call x1, Pallas kernels, fused_shards(): pl.pallas_call(functools.partial(fused_kernel, segs, vids, tps), out_shap...  54.5 us
    unnamed x2, local copies, waits for them, and re-layouts  1.77 us

profile of v3, /device:TPU:0, one launch (start us, length us, event | category | flops | bytes accessed | tf_op | source)
XLA Modules:
  0.0 56.9 jit_solution(17152354828017571410)
XLA Ops:
  0.6 54.5 %shard_map.77 = (bf16[512,1024]{1,0:T(8,128)(2,1)S(1)}, f32[128,1024]{1,0:T(8,128)S(1)}) custom-call(bf16[512,1024]{1,0:T(8,128)(2,1)} %bitcast.9, bf16[4,128,1024]{2,1,0:T(8,128)(2,1)} %bitcast.10, bf16[4,128,1024]{2,1,0:T(8,128)(2,1)} %bitcast.11, bf16[128,1024]{1,0:T(8,128)(2,1)} %latent_in.1, f32[128,1024]{1,0:T(8,128)} %bitcast.12, f32[1,1024]{1,0:T(1,128)} %bitcast.13), custom_call_target="tpu_custom_call" | custom-call | tf_op jit(solution)/shard_map/pallas_call | solution.py:429
  55.1 1.0 %copy.10 = bf16[1,512,1024]{2,1,0:T(8,128)(2,1)} copy(bf16[1,512,1024]{2,1,0:T(8,128)(2,1)S(1)} %bitcast.7) | data formatting | bytes 2097152
  56.1 0.8 %copy.11 = f32[1,128,1024]{2,1,0:T(8,128)} copy(f32[1,128,1024]{2,1,0:T(8,128)S(1)} %bitcast.8) | data formatting | bytes 1048576

commit v4 on v3

--- a/solution.py
+++ b/solution.py
@@ -370,7 +370,7 @@
             place(mixed_at + lag, carry, k, seg)
     for k in range(tiles, 2 * tiles):
         place(done[k], query, k)
-        place(max(done[k], mixed_at + LAGS[-1]), readout, k)
+        place(max(done[k // 2 * 2 + 1], mixed_at + LAGS[-1]), readout, k)
     for at, slot in enumerate(slots):
         place(at - 0.2, arrive_z, *slot)
     for at, slot in relays:

time: 57.1 us -> 57.1 us (level)
  no operation moved by 1% of the time
where the time goes in v4:
time: 57.1 us; the launch traced here: 56.9 us
  Pallas kernels  54.5 us (95%)
  local copies, waits for them, and re-layouts  1.77 us (3%)
  between operations  0.64 us (1%)
    pallas_call x1, Pallas kernels, fused_shards(): pl.pallas_call(functools.partial(fused_kernel, segs, vids, tps), out_shap...  54.5 us
    unnamed x2, local copies, waits for them, and re-layouts  1.77 us

profile of v4, /device:TPU:0, one launch (start us, length us, event | category | flops | bytes accessed | tf_op | source)
XLA Modules:
  0.0 56.9 jit_solution(17152354828017571410)
XLA Ops:
  0.6 54.5 %shard_map.77 = (bf16[512,1024]{1,0:T(8,128)(2,1)S(1)}, f32[128,1024]{1,0:T(8,128)S(1)}) custom-call(bf16[512,1024]{1,0:T(8,128)(2,1)} %bitcast.9, bf16[4,128,1024]{2,1,0:T(8,128)(2,1)} %bitcast.10, bf16[4,128,1024]{2,1,0:T(8,128)(2,1)} %bitcast.11, bf16[128,1024]{1,0:T(8,128)(2,1)} %latent_in.1, f32[128,1024]{1,0:T(8,128)} %bitcast.12, f32[1,1024]{1,0:T(1,128)} %bitcast.13), custom_call_target="tpu_custom_call" | custom-call | tf_op jit(solution)/shard_map/pallas_call | solution.py:429
  55.1 1.0 %copy.10 = bf16[1,512,1024]{2,1,0:T(8,128)(2,1)} copy(bf16[1,512,1024]{2,1,0:T(8,128)(2,1)S(1)} %bitcast.7) | data formatting | bytes 2097152
  56.1 0.8 %copy.11 = f32[1,128,1024]{2,1,0:T(8,128)} copy(f32[1,128,1024]{2,1,0:T(8,128)S(1)} %bitcast.8) | data formatting | bytes 1048576
